TPU v7x, 768 devices: a whole 4x8x12 slice. The times are simulated.
768 devices in a mesh: rows: 64 (over x, y, core), cols: 12 (over z).
Axes of the slice: x: 4, y: 8, z: 12, core: 2. Of those that a mesh axis runs over, the one named last changes fastest.
Arguments:
- basis: bfloat16 [786432, 512], P(('rows', 'cols')), may hold values from -6 to 6
- blocks: bfloat16 [6144, 8, 128, 128], P(('rows', 'cols')), may hold values from -0.1875 to 0.1875
- neighbours: int32 [6144, 8], P(('rows', 'cols')), may hold values from 0 to 6143, as said below
- counts: int32 [6144], P(('rows', 'cols')), may hold values from 3 to 8
- rotation: bfloat16 [512, 256], replicated, may hold values from -0.25 to 0.25
- ritz_values: float32 [256], replicated, may hold values from -2 to 2
Outputs:
- ritz: bfloat16 [786432, 256], P(('rows', 'cols'))
- ritz_image: bfloat16 [786432, 256], P(('rows', 'cols'))
- gram: float32 [512, 512], P('rows')
- projected: float32 [512, 512], P('rows')
- res_norm: float32 [256], replicated
Inputs may be any that keep to these rules, and one draw needn't show every extreme that they name: `neighbours`: every entry of row block b lies among the blocks of b's device and the one block just before and just after them: from 8 * (b // 8) - 1 to 8 * (b // 8) + 8; slot 0 is b itself; entries may repeat; entries at slots from counts[b] on are padding. `counts`: at least three slots are live.
All inputs are finite; a program needn't handle non-finite values.
Results may differ from a plain program's by a relative error of at most 0.015.
Values may be sent and summed in bfloat16 or wider, within the bound.
No kernel may reach another device: no remote copies, remote signals or barrier semaphores. Data moves between devices by JAX's collectives and lax.ppermute only.
A program may use at most 64 MiB of HBM per device.

v0:
```python
import jax
import jax.numpy as jnp
from jax import lax
from jax.sharding import Mesh
from jax.sharding import PartitionSpec as P

ROWS = ("rows_0", "rows_1", "rows_2")
ROWS_COLS = ("rows_0", "rows_1", "rows_2", "cols")


def extended(block, sides, width):
    for axis, dim in sides:
        count = lax.axis_size(axis)
        forward = [(i, i + 1) for i in range(count - 1)]
        backward = [(target, source) for source, target in forward]
        low = lax.ppermute(
            lax.slice_in_dim(block, block.shape[dim] - width, None, axis=dim), axis, forward
        )
        high = lax.ppermute(lax.slice_in_dim(block, 0, width, axis=dim), axis, backward)
        block = jnp.concatenate([low, block, high], axis=dim)
    return block


def split_up(x, dim, peers):
    before, after = (x.shape[:dim], x.shape[dim + 1 :])
    return jnp.moveaxis(x.reshape(*before, peers, -1, *after), dim, 0)


def summed_on_arrival(x, axis, dim):
    blocks = split_up(x, dim, lax.axis_size(axis))
    arrived = lax.all_to_all(blocks, axis, split_axis=0, concat_axis=0, tiled=True)
    return arrived.sum(axis=0)


def over_pieces(x, axis):
    return lax.all_gather(x, axis).astype(jnp.float32).sum(0)


def by_axis(x, axes):
    for axis in axes:
        x = lax.psum(x, axis)
    return x


def body(basis, blocks, neighbours, counts, rotation, ritz_values):
    count_blocks = blocks.shape[0]
    slots = blocks.shape[1]
    size_block = blocks.shape[2]
    width = basis.shape[1]
    devices = lax.axis_size(ROWS) * lax.axis_size("cols")
    rows_total = basis.shape[0] * devices
    first = lax.axis_index(ROWS_COLS) * count_blocks - 1
    local_index = neighbours - first
    live = jnp.arange(slots, dtype=jnp.int32)[None, :] < counts[:, None]
    masked = jnp.where(live[:, :, None, None], blocks, jnp.zeros_like(blocks))
    total = jnp.zeros((count_blocks, size_block, width), jnp.float32)
    own = basis.reshape(count_blocks, size_block, width)
    inside = (local_index >= 1) & (local_index <= count_blocks)
    for slot in range(slots):
        picked = own[jnp.clip(local_index[:, slot] - 1, 0, count_blocks - 1)]
        held = jnp.where(
            inside[:, slot][:, None, None], masked[:, slot], jnp.zeros_like(masked[:, slot])
        )
        total = total + jnp.einsum("brs,bsk->brk", held, picked, preferred_element_type=jnp.float32)
    padded = extended(basis, ((ROWS_COLS, 0),), size_block)
    lower_rows = padded[:size_block]
    upper_rows = padded[-size_block:]
    zero_block = jnp.zeros_like(masked)
    below = jnp.sum(jnp.where((local_index == 0)[:, :, None, None], masked, zero_block), axis=1)
    above = jnp.sum(
        jnp.where((local_index == count_blocks + 1)[:, :, None, None], masked, zero_block), axis=1
    )
    total = total + jnp.einsum("brs,sk->brk", below, lower_rows, preferred_element_type=jnp.float32)
    total = total + jnp.einsum("brs,sk->brk", above, upper_rows, preferred_element_type=jnp.float32)
    image = total.reshape(basis.shape[0], width).astype(jnp.bfloat16)
    joined = jnp.concatenate([basis, image], axis=1)
    partial_rows = summed_on_arrival(
        jnp.dot(basis.T, joined, preferred_element_type=jnp.float32) / rows_total, ROWS, 0
    )
    both = over_pieces(partial_rows.astype(jnp.bfloat16), "cols").astype(jnp.float32)
    gram = both[:, :width]
    projected = both[:, width:]
    ritz_full = jnp.dot(basis, rotation, preferred_element_type=jnp.float32)
    image_full = jnp.dot(image, rotation, preferred_element_type=jnp.float32)
    resid = image_full - ritz_values[None, :] * ritz_full
    squares = by_axis(jnp.sum(resid * resid, axis=0), ROWS_COLS)
    res_norm = jnp.sqrt(squares / rows_total)
    return (
        ritz_full.astype(jnp.bfloat16),
        image_full.astype(jnp.bfloat16),
        gram,
        projected,
        res_norm,
    )


def solution(mesh):
    finer = Mesh(
        mesh.devices.reshape(4, 8, 2, mesh.shape["cols"]), ("rows_0", "rows_1", "rows_2", "cols")
    )
    return jax.shard_map(
        body,
        mesh=finer,
        in_specs=(
            P(ROWS_COLS, None),
            P(ROWS_COLS, None, None, None),
            P(ROWS_COLS, None),
            P(ROWS_COLS),
            P(),
            P(),
        ),
        out_specs=(P(ROWS_COLS, None), P(ROWS_COLS, None), P(ROWS, None), P(ROWS, None), P()),
        check_vma=False,
    )
```

profile of v0, /device:TPU:6, one launch (start us, length us, event | category | flops | bytes accessed | tf_op | source)
XLA Modules:
  0.0 166.9 jit_solution(4590041887873636581)
XLA Ops:
  0.6 0.0 copy-start
  0.6 0.0 copy-start.1
  0.7 1.8 %fusion.69 = (bf16[128,512]{1,0:T(8,128)(2,1)}, bf16[128,512]{1,0:T(8,128)(2,1)}) fusion(bf16[1024,512]{1,0:T(8,128)(2,1)} %param.6), kind=kLoop, calls=%fused_computation.110 | loop fusion | bytes 524288 | tf_op jit(solution)/shard_map/slice | solution.py:19
  2.4 4.3 %collective-permute-start = (bf16[128,512]{1,0:T(8,128)(2,1)}, bf16[128,512]{1,0:T(8,128)(2,1)}, u32[]{:S(2)}, u32[]{:S(2)}) collective-permute-start(bf16[128,512]{1,0:T(8,128)(2,1)} %get-tuple-element.30), channel_id=1, source_target_pairs={{0,1},{1,2},{2,3},{3,4},{4,5},{5,6},{6,7},{7,8},{8,9},{9,10},{10,1... | collective-permute-start | bytes 393224 | tf_op jit(solution)/shard_map/ppermute | solution.py:16
  6.7 14.8 %collective-permute-start.1 = (bf16[128,512]{1,0:T(8,128)(2,1)}, bf16[128,512]{1,0:T(8,128)(2,1)S(1)}, u32[]{:S(2)}, u32[]{:S(2)}) collective-permute-start(bf16[128,512]{1,0:T(8,128)(2,1)} %get-tuple-element.29), channel_id=1, source_target_pairs={{1,0},{2,1},{3,2},{4,3},{5,4},{6,5},{7,6},{8,7},{9,8},{10,9},{11,1... | collective-permute-start | bytes 393224 | tf_op jit(solution)/shard_map/ppermute | solution.py:19
  21.6 0.7 compare_and_fusion
  22.3 0.8 fusion.53
  23.1 1.3 broadcast_compare_fusion.1
  24.4 0.8 slice_reduce_fusion.6
  25.2 1.8 %gather_fusion.6 = bf16[8,128,512]{2,1,0:T(8,128)(2,1)S(1)} fusion(bf16[8,128,512]{2,1,0:T(8,128)(2,1)} %bitcast.86, s32[1024]{0:T(1024)S(1)} %get-tuple-element.38), kind=kCustom, calls=%fused_computation.6 | custom fusion | bytes 2097184 | tf_op jit(solution)/shard_map/gather | solution.py:60
  27.1 0.6 gather_fusion.5
  27.7 1.6 gather_fusion.4
  29.3 0.6 pad_clamp_fusion.4
  29.9 1.6 gather_fusion.3
  31.6 1.6 gather_fusion.2
  33.2 0.7 pad_clamp_fusion.6
  33.8 1.6 gather_fusion.1
  35.4 1.6 gather_fusion
  37.1 1.6 gather_fusion.7
  38.7 0.0 copy-done.11
  38.7 2.8 %select_reduce_fusion = (bf16[8,128,128]{2,1,0:T(8,128)(2,1)S(1)}, bf16[8,128,128]{2,1,0:T(8,128)(2,1)S(1)}, bf16[8,8,128,128]{3,2,1,0:T(8,128)(2,1)S(1)}) fusion(pred[8,8]{1,0:T(8,128)(4,1)S(1)} %copy-done.10, pred[8,8]{1,0:T(8,128)(4,1)S(1)} %get-tuple-element.33, bf16[8,8,128,128]{3,2,1,0:T(8,128)(2,1)} %param.7, pred[8,8]{1,0:T(8,128)(4,1)S(1)} %copy-done.11), kind=kLoop, calls=%fused_computation.14 | loop fusion | flops 4980736 | bytes 4718784 | tf_op jit(solution)/shard_map/reduce_sum | solution.py:70
  41.5 0.0 copy-start.18
  41.5 0.0 copy-done.19
  41.5 0.5 fusion.10
  42.0 0.0 copy-start.4
  42.0 0.0 copy-start.17
  42.0 0.1 copy-done.18
  42.1 0.5 fusion.13
  42.6 0.6 copy-done.4
  43.2 0.0 copy-done.17
  43.2 0.5 fusion.16
  43.7 0.2 copy-done.5
  43.9 0.5 fusion.19
  44.4 0.6 copy-done.6
  45.0 0.5 fusion.22
  45.4 0.2 copy-done.8
  45.6 0.5 fusion.25
  46.1 0.6 copy-done.9
  46.7 0.5 fusion.28
  47.2 0.2 copy-done.7
  47.4 0.0 copy-done.12
  47.4 0.5 fusion.7
  47.9 0.0 collective-permute-done
  47.9 1.3 fusion.42
  49.2 0.0 collective-permute-done.1
  49.2 0.9 add_convert_fusion
  50.2 0.0 copy-start.2
  50.2 1.0 copy-done.2
  51.2 2.6 %multiply_bitcast_fusion = f32[64,8,1024]{2,1,0:T(8,128)} fusion(bf16[1024,512]{1,0:T(8,128)(2,1)S(1)} %copy-done.1, bf16[1024,512]{1,0:T(8,128)(2,1)S(1)} %bitcast.94), kind=kOutput, calls=%fused_computation.12 | convolution fusion | flops 1078460416 | bytes 4194304 | tf_op jit(solution)/shard_map/dot_general | solution.py:78
  53.8 7.9 %all-to-all-start = ((f32[64,8,1024]{2,1,0:T(8,128)}), f32[64,8,1024]{2,1,0:T(8,128)S(1)}, u32[]{:S(2)}, u32[]{:S(2)}) async-start(f32[64,8,1024]{2,1,0:T(8,128)} %multiply_bitcast_fusion), calls=%async_computation | async-start | bytes 4194304 | tf_op jit(solution)/shard_map/all_to_all | solution.py:31
  61.7 0.0 copy-done
  61.8 0.0 copy-start.20
  61.8 0.4 fusion.71
  62.2 0.8 copy-done.3
  63.0 1.4 multiply_reduce_fusion
  64.4 7.7 %psum.28 = f32[256]{0:T(256)S(1)} all-reduce(f32[256]{0:T(256)S(1)} %get-tuple-element.26), channel_id=1, replica_groups=mesh['rows_0'=4,'rows_1'=8,'rows_2'=2,'cols'=12] {'rows_0'}, use_global_device_ids=true, to_apply=%region_5.6 | all-reduce | flops 256 | bytes 2048 | tf_op jit(solution)/shard_map/psum | solution.py:41
  72.1 47.4 %psum.29 = f32[256]{0:T(256)S(1)} all-reduce(f32[256]{0:T(256)S(1)} %psum.28), channel_id=1, replica_groups=mesh['rows_0'=4,'rows_1'=8,'rows_2'=2,'cols'=12] {'rows_1'}, use_global_device_ids=true, to_apply=%region_6.7 | all-reduce | flops 256 | bytes 2048 | tf_op jit(solution)/shard_map/psum | solution.py:41
  119.5 2.5 %psum.30 = f32[256]{0:T(256)S(1)} all-reduce(f32[256]{0:T(256)S(1)} %psum.29), channel_id=1, replica_groups=mesh['rows_0'=4,'rows_1'=8,'rows_2'=2,'cols'=12] {'rows_2'}, use_global_device_ids=true, to_apply=%region_7.8 | all-reduce | flops 256 | bytes 2048 | tf_op jit(solution)/shard_map/psum | solution.py:41
  122.0 22.9 %psum.31 = f32[256]{0:T(256)S(1)} all-reduce(f32[256]{0:T(256)S(1)} %psum.30), channel_id=1, replica_groups=mesh['rows_0'=4,'rows_1'=8,'rows_2'=2,'cols'=12] {'cols'}, use_global_device_ids=true, to_apply=%region_8.9 | all-reduce | flops 256 | bytes 2048 | tf_op jit(solution)/shard_map/psum | solution.py:41
  144.9 0.6 multiply_sqrt_fusion
  145.5 0.0 all-to-all-done
  145.5 0.1 reduce_sum.53
  145.6 20.6 %all-gather = bf16[96,1024]{1,0:T(8,128)(2,1)S(1)} all-gather(bf16[8,1024]{1,0:T(8,128)(2,1)S(1)} %reduce_sum.53), channel_id=2, replica_groups=mesh['rows_0'=4,'rows_1'=8,'rows_2'=2,'cols'=12] {'cols'}, dimensions={0}, use_global_device_ids=true | all-gather | bytes 212992 | tf_op jit(solution)/shard_map/all_gather | solution.py:36
  166.3 0.6 fusion.70
  (24 shorter events, 0.1 us)
Async XLA Ops:
  0.6 61.1 %copy-start = (bf16[512,256]{1,0:T(8,128)(2,1)S(1)}, bf16[512,256]{1,0:T(8,128)(2,1)}, u32[]{:S(2)}) copy-start(bf16[512,256]{1,0:T(8,128)(2,1)} %param.10) | copy-start | bytes 786436
  0.6 26.5 %copy-start.1 = (bf16[1024,512]{1,0:T(8,128)(2,1)S(1)}, bf16[1024,512]{1,0:T(8,128)(2,1)}, u32[]{:S(2)}) copy-start(bf16[1024,512]{1,0:T(8,128)(2,1)} %param.6) | copy-start | bytes 3145732
  2.4 45.5 %collective-permute-start = (bf16[128,512]{1,0:T(8,128)(2,1)}, bf16[128,512]{1,0:T(8,128)(2,1)}, u32[]{:S(2)}, u32[]{:S(2)}) collective-permute-start(bf16[128,512]{1,0:T(8,128)(2,1)} %get-tuple-element.30), channel_id=1, source_target_pairs={{0,1},{1,2},{2,3},{3,4},{4,5},{5,6},{6,7},{7,8},{8,9},{9,10},{10,1... | collective-permute-start | bytes 393224 | tf_op jit(solution)/shard_map/ppermute | solution.py:16
  6.7 42.5 %collective-permute-start.1 = (bf16[128,512]{1,0:T(8,128)(2,1)}, bf16[128,512]{1,0:T(8,128)(2,1)S(1)}, u32[]{:S(2)}, u32[]{:S(2)}) collective-permute-start(bf16[128,512]{1,0:T(8,128)(2,1)} %get-tuple-element.29), channel_id=1, source_target_pairs={{1,0},{2,1},{3,2},{4,3},{5,4},{6,5},{7,6},{8,7},{9,8},{10,9},{11,1... | collective-permute-start | bytes 393224 | tf_op jit(solution)/shard_map/ppermute | solution.py:19
  35.4 3.3 %copy-start.10 = (pred[8,8]{1,0:T(8,128)(4,1)S(1)}, pred[8,8]{1,0:T(8,128)(4,1)}, u32[]{:S(2)}) copy-start(pred[8,8]{1,0:T(8,128)(4,1)} %get-tuple-element.34) | copy-start | bytes 196
  37.1 1.6 copy-start.11
  38.7 2.8 %copy-start.19 = (pred[8]{0:T(512)(128)(4,1)S(1)}, pred[8]{0:T(512)(128)(4,1)}, u32[]{:S(2)}) copy-start(pred[8]{0:T(512)(128)(4,1)} %get-tuple-element.17) | copy-start | bytes 28
  41.5 0.6 copy-start.18
  42.0 1.2 copy-start.4
  42.0 1.2 copy-start.17
  42.5 1.3 copy-start.5
  42.6 1.3 copy-start.16
  43.7 1.3 copy-start.6
  43.7 1.3 copy-start.15
  44.3 1.3 copy-start.8
  44.3 1.3 copy-start.14
  45.4 1.3 copy-start.9
  45.4 1.3 copy-start.13
  46.1 1.3 copy-start.7
  46.1 1.3 copy-start.12
  50.2 1.0 copy-start.2
  53.8 91.6 %all-to-all-start = ((f32[64,8,1024]{2,1,0:T(8,128)}), f32[64,8,1024]{2,1,0:T(8,128)S(1)}, u32[]{:S(2)}, u32[]{:S(2)}) async-start(f32[64,8,1024]{2,1,0:T(8,128)} %multiply_bitcast_fusion), calls=%async_computation | async-start | bytes 4194304 | tf_op jit(solution)/shard_map/all_to_all | solution.py:31
  61.8 1.2 copy-start.3
  61.8 1.2 copy-start.20
where the time goes:
time: 168 us; the launch traced here: 167 us
  blocking collectives  101 us (60%)
  starting transfers between devices  27 us (16%)
  local copies, waits for them, and re-layouts  19.6 us (12%)
  matrix products  10.5 us (6%)
  other arithmetic  7.64 us (5%)
    psum x4, blocking collectives, by_axis(): x = lax.psum(x, axis)  80.5 us
    all_gather x1, blocking collectives, over_pieces(): return lax.all_gather(x, axis).astype(jnp.float32).sum(0)  20.6 us
    ppermute x1, starting transfers between devices, extended(): lax.ppermute(lax.slice_in_dim(block, 0, width, axis=dim), axis, backward)  14.8 us
    gather x8, local copies, waits for them, and re-layouts, body(): picked = own[jnp.clip(local_index[:, slot] - 1, 0, count_blocks - 1)]  12.1 us
    all_to_all x1, starting transfers between devices, summed_on_arrival(): lax.all_to_all(blocks, axis, split_axis=0, concat_axis=0, tiled=True)  7.91 us
    unnamed x42, local copies, waits for them, and re-layouts  4.29 us
    ppermute x1, starting transfers between devices, extended(): lax.ppermute(lax.slice_in_dim(block, block.shape[dim] - width, None, axis...  4.27 us
    dot_general x8, matrix products, body(): jnp.einsum('brs,bsk->brk', held, picked, preferred_element_type=jnp.float32)  3.79 us
  transfers between devices with their start and end apart: 3, of which 0 were waited for; matrix products, arithmetic and copies ran while one was open for 16% of the time, Pallas kernels for 0%

commit v1 on v0

v1 whole, which is shorter than its diff:
```python
import jax
import jax.numpy as jnp
from jax import lax
from jax.experimental import pallas as pl
from jax.experimental.pallas import tpu as pltpu
from jax.sharding import Mesh
from jax.sharding import PartitionSpec as P

ROWS = ("rows_0", "rows_1", "rows_2")
ROWS_COLS = ("rows_0", "rows_1", "rows_2", "cols")
LANES = 128
F32 = jnp.float32
BF16 = jnp.bfloat16


def dot(a, b):
    return jnp.dot(a, b, preferred_element_type=F32)


def store_tiles(out_ref, acc_ref, nx, ny, nc, first, per_group):
    tiles = acc_ref.shape[1] // LANES
    for x in range(nx):
        for y in range(ny):
            for c in range(nc):
                row = ((x * ny + y) * nc + c) * 8
                for j in range(0, tiles, 2):
                    pair = jnp.concatenate(
                        [
                            acc_ref[row : row + 8, j * LANES : (j + 1) * LANES],
                            acc_ref[row : row + 8, (j + 1) * LANES : (j + 2) * LANES],
                        ],
                        axis=0,
                    )
                    at = (y * per_group + first + j) * 8
                    out_ref[x * nc + c, at : at + 16, :] = pair.astype(BF16)


def early_kernel(nx, ny, nc, basis_ref, rot_ref, basis_t_ref, gram_ref, ritz_ref, acc_ref):
    basis_t_ref[...] = basis_ref[...].T
    acc_ref[...] = dot(basis_t_ref[...], basis_ref[...])
    store_tiles(gram_ref, acc_ref, nx, ny, nc, 0, acc_ref.shape[1] // LANES)
    ritz_ref[...] = dot(basis_ref[...], rot_ref[...]).astype(BF16)


def late_kernel(
    nx, ny, nc,
    neighbours_ref, counts_ref, blocks_ref, basis_ref, low_ref, high_ref, basis_t_ref, gram_ref,
    rot_ref, values_ref, out_ref, ritz_image_ref, padded_ref, image_ref, acc_ref,
):
    nb, slots, size, _ = blocks_ref.shape
    rows, width = basis_ref.shape
    padded_ref[0:size, :] = low_ref[...]
    padded_ref[size : size + rows, :] = basis_ref[...]
    padded_ref[size + rows :, :] = high_ref[...]
    first = neighbours_ref[0, 0] - 1
    for b in range(nb):
        total = None
        for j in range(0, slots, 2):
            held = []
            picked = []
            for s in (j, j + 1):
                block = blocks_ref[b, s]
                held.append(jnp.where(s < counts_ref[b], block, jnp.zeros_like(block)))
                index = jnp.clip(neighbours_ref[b, s] - first, 0, nb + 1)
                picked.append(padded_ref[pl.ds(pl.multiple_of(index * size, size), size), :])
            part = dot(jnp.concatenate(held, axis=1), jnp.concatenate(picked, axis=0))
            total = part if total is None else total + part
        image_ref[b * size : (b + 1) * size, :] = total.astype(BF16)
    acc_ref[...] = dot(basis_t_ref[...], image_ref[...])
    tiles = width // LANES
    for g in range(nx * nc):
        for y in range(ny):
            at = y * 2 * tiles * 8
            out_ref[g, at : at + tiles * 8, :] = gram_ref[g, y * tiles * 8 : (y + 1) * tiles * 8, :]
    store_tiles(out_ref, acc_ref, nx, ny, nc, tiles, 2 * tiles)
    image_full = dot(image_ref[...], rot_ref[...])
    ritz_image_ref[...] = image_full.astype(BF16)
    resid = image_full - values_ref[...] * dot(basis_ref[...], rot_ref[...])
    squares = jnp.sum(resid * resid, axis=0, keepdims=True)
    parts = squares.shape[1] // LANES
    line = lax.broadcasted_iota(jnp.int32, (16, LANES), 0)
    spread = jnp.zeros((16, LANES), F32)
    for p in range(parts):
        spread = jnp.where(line == p, squares[:, p * LANES : (p + 1) * LANES], spread)
    end = 2 * tiles * 8 * ny
    for g in range(nx * nc):
        out_ref[g, end : end + 16, :] = spread.astype(BF16)


def sum_groups(in_ref):
    total = in_ref[0].astype(F32)
    for i in range(1, in_ref.shape[0]):
        total = total + in_ref[i].astype(F32)
    return total


def split_kernel(in_ref, out_ref):
    total = sum_groups(in_ref).astype(BF16)
    ny = out_ref.shape[0]
    each = out_ref.shape[1] - 16
    for y in range(ny):
        out_ref[y, 0:each, :] = total[y * each : (y + 1) * each]
        out_ref[y, each : each + 16, :] = total[ny * each :]


def repeat_kernel(in_ref, out_ref):
    total = sum_groups(in_ref).astype(BF16)
    for i in range(out_ref.shape[0]):
        out_ref[i] = total


def final_kernel(rows_total, in_ref, gram_ref, projected_ref, res_ref):
    total = sum_groups(in_ref) / rows_total
    tiles = gram_ref.shape[1] // LANES
    for j in range(tiles):
        gram_ref[:, j * LANES : (j + 1) * LANES] = total[j * 8 : (j + 1) * 8]
        projected_ref[:, j * LANES : (j + 1) * LANES] = total[(tiles + j) * 8 : (tiles + j + 1) * 8]
    res_ref[...] = jnp.sqrt(total[2 * tiles * 8 : 2 * tiles * 8 + res_ref.shape[0]])


def halos(basis, width):
    count = lax.axis_size(ROWS_COLS)
    forward = [(i, i + 1) for i in range(count - 1)]
    backward = [(target, source) for source, target in forward]
    low = lax.ppermute(basis[basis.shape[0] - width :], ROWS_COLS, forward)
    high = lax.ppermute(basis[:width], ROWS_COLS, backward)
    return low, high


def exchanged(x, axes):
    return lax.all_to_all(x, axes, split_axis=0, concat_axis=0, tiled=True)


def shape(dims, dtype):
    return jax.ShapeDtypeStruct(dims, dtype)


def body(basis, blocks, neighbours, counts, rotation, ritz_values):
    rows, width = basis.shape
    size = blocks.shape[2]
    kept = rotation.shape[1]
    nx, ny, nc = (lax.axis_size(axis) for axis in ROWS)
    nz = lax.axis_size("cols")
    rows_total = rows * nx * ny * nc * nz
    tiles = width // LANES
    groups = nx * nc
    vmem = pl.BlockSpec(memory_space=pltpu.VMEM)
    smem = pl.BlockSpec(memory_space=pltpu.SMEM)
    low, high = halos(basis, size)
    basis_t, gram_part, ritz = pl.pallas_call(
        lambda *refs: early_kernel(nx, ny, nc, *refs),
        out_shape=(
            shape((width, rows), BF16),
            shape((groups, ny * tiles * 8, LANES), BF16),
            shape((rows, kept), BF16),
        ),
        in_specs=[vmem] * 2,
        out_specs=(vmem,) * 3,
        scratch_shapes=[pltpu.VMEM((width, width), F32)],
        cost_estimate=pl.CostEstimate(
            flops=2 * rows * width * (width + kept), bytes_accessed=4 * rows * width * 2, transcendentals=0
        ),
        name="early",
    )(basis, rotation)
    payload, ritz_image = pl.pallas_call(
        lambda *refs: late_kernel(nx, ny, nc, *refs),
        out_shape=(
            shape((groups, ny * 2 * tiles * 8 + 16, LANES), BF16),
            shape((rows, kept), BF16),
        ),
        in_specs=[smem, smem] + [vmem] * 8,
        out_specs=(vmem,) * 2,
        scratch_shapes=[
            pltpu.VMEM((rows + 2 * size, width), BF16),
            pltpu.VMEM((rows, width), BF16),
            pltpu.VMEM((width, width), F32),
        ],
        cost_estimate=pl.CostEstimate(
            flops=4 * rows * width * 1024, bytes_accessed=8 * rows * width * 2, transcendentals=0
        ),
        name="late",
    )(
        neighbours, counts, blocks, basis, low, high, basis_t, gram_part, rotation,
        ritz_values.reshape(1, kept),
    )
    arrived = exchanged(payload, ("rows_0", "rows_2"))
    each = 2 * tiles * 8 + 16
    split = pl.pallas_call(
        split_kernel,
        out_shape=shape((ny, each, LANES), BF16),
        in_specs=[vmem],
        out_specs=vmem,
        name="split",
    )(arrived)
    repeated = pl.pallas_call(
        repeat_kernel,
        out_shape=shape((nz, each, LANES), BF16),
        in_specs=[vmem],
        out_specs=vmem,
        name="repeated",
    )(exchanged(split, "rows_1"))
    gram, projected, res = pl.pallas_call(
        lambda *refs: final_kernel(rows_total, *refs),
        out_shape=(
            shape((8, width), F32),
            shape((8, width), F32),
            shape((kept // LANES, LANES), F32),
        ),
        in_specs=[vmem],
        out_specs=(vmem,) * 3,
        name="final",
    )(exchanged(repeated, "cols"))
    return ritz, ritz_image, gram, projected, res.reshape(kept)


def solution(mesh):
    finer = Mesh(
        mesh.devices.reshape(4, 8, 2, mesh.shape["cols"]), ("rows_0", "rows_1", "rows_2", "cols")
    )
    return jax.shard_map(
        body,
        mesh=finer,
        in_specs=(
            P(ROWS_COLS, None),
            P(ROWS_COLS, None, None, None),
            P(ROWS_COLS, None),
            P(ROWS_COLS),
            P(),
            P(),
        ),
        out_specs=(P(ROWS_COLS, None), P(ROWS_COLS, None), P(ROWS, None), P(ROWS, None), P()),
        check_vma=False,
    )
```

time: 168 us -> 94.3 us (0.56)
  blocking collectives: 101 us -> 51.5 us
  local copies, waits for them, and re-layouts: 19.6 us -> 1.65 us
  Pallas kernels: 0 us -> 14.4 us
  matrix products: 10.5 us -> 0 us
  starting transfers between devices: 27 us -> 19.1 us
  other arithmetic: 7.64 us -> 0 us
  waiting for transfers between devices: 0.01 us -> 5.45 us
    psum x4 -> x0, blocking collectives: 80.5 us -> none  [by_axis(): x = lax.psum(x, axis)]
    all_to_all x0 -> x3, blocking collectives: none -> 51.5 us  [exchanged(): return lax.all_to_all(x, axes, split_axis=0, concat_axis=0, tiled=True)]
    all_gather x1 -> x0, blocking collectives: 20.6 us -> none  [over_pieces(): return lax.all_gather(x, axis).astype(jnp.float32).sum(0)]
    pallas_call x0 -> x5, Pallas kernels: none -> 14.4 us  [the longest x1 6.04 us: body(): pl.pallas_call(lambda *refs: late_kernel(nx, ny, nc, *refs), out_shape=(s...]
    gather x8 -> x0, local copies, waits for them, and re-layouts: 12.1 us -> none  [body(): picked = own[jnp.clip(local_index[:, slot] - 1, 0, count_blocks - 1)]]
    dot_general x13 -> x0, matrix products: 10.5 us -> none  [the longest x8 3.79 us: body(): jnp.einsum('brs,bsk->brk', held, picked, preferred_element_type=jnp.float32)]
    all_to_all x1 -> x0, starting transfers between devices: 7.91 us -> none  [summed_on_arrival(): lax.all_to_all(blocks, axis, split_axis=0, concat_axis=0, tiled=True)]
    ppermute x2, waiting for transfers between devices: 0.01 us -> 5.45 us  [the longest x1 5.45 us: halos(): low = lax.ppermute(basis[basis.shape[0] - width:], ROWS_COLS, forward)]
  transfers between devices with their start and end apart: 3 -> 2, of which waited for: 0 -> 1; matrix products, arithmetic and copies ran while one was open for 16% -> 0% of each run, Pallas kernels for 0% -> 3%
where the time goes in v1:
time: 94.3 us; the launch traced here: 92.8 us
  blocking collectives  51.5 us (55%)
  starting transfers between devices  19.1 us (20%)
  Pallas kernels  14.4 us (15%)
  waiting for transfers between devices  5.45 us (6%)
  local copies, waits for them, and re-layouts  1.65 us (2%)
    all_to_all x3, blocking collectives, exchanged(): return lax.all_to_all(x, axes, split_axis=0, concat_axis=0, tiled=True)  51.5 us
    ppermute x1, starting transfers between devices, halos(): high = lax.ppermute(basis[:width], ROWS_COLS, backward)  17.2 us
    pallas_call x1, Pallas kernels, body(): pl.pallas_call(lambda *refs: late_kernel(nx, ny, nc, *refs), out_shape=(s...  6.04 us
    ppermute x1, waiting for transfers between devices, halos(): low = lax.ppermute(basis[basis.shape[0] - width:], ROWS_COLS, forward)  5.45 us
    pallas_call x1, Pallas kernels, body(): pl.pallas_call(lambda *refs: early_kernel(nx, ny, nc, *refs), out_shape=(...  3.12 us
    pallas_call x1, Pallas kernels, body(): pl.pallas_call(split_kernel, out_shape=shape((ny, each, LANES), BF16), in...  2.03 us
    ppermute x1, starting transfers between devices, halos(): low = lax.ppermute(basis[basis.shape[0] - width:], ROWS_COLS, forward)  1.92 us
  transfers between devices with their start and end apart: 2, of which 1 were waited for; matrix products, arithmetic and copies ran while one was open for 0% of the time, Pallas kernels for 3%

profile of v1, /device:TPU:6, one launch (start us, length us, event | category | flops | bytes accessed | tf_op | source)
XLA Modules:
  0.0 92.8 jit_solution(5290566632241996179)
XLA Ops:
  0.6 1.0 %fusion = (bf16[128,512]{1,0:T(8,128)(2,1)S(1)}, bf16[128,512]{1,0:T(8,128)(2,1)S(1)}) fusion(bf16[1024,512]{1,0:T(8,128)(2,1)} %refs_3_.1), kind=kLoop, calls=%fused_computation | loop fusion | bytes 524288 | tf_op jit(solution)/shard_map/slice | solution.py:126
  1.6 17.2 %collective-permute-start.1 = (bf16[128,512]{1,0:T(8,128)(2,1)S(1)}, bf16[128,512]{1,0:T(8,128)(2,1)S(1)}, u32[]{:S(2)}, u32[]{:S(2)}) collective-permute-start(bf16[128,512]{1,0:T(8,128)(2,1)S(1)} %get-tuple-element.21), channel_id=1, source_target_pairs={{1,0},{2,1},{3,2},{4,3},{5,4},{6,5},{7,6},{8,7},{9,8},{10,9},{11,1... | collective-permute-start | bytes 393224 | tf_op jit(solution)/shard_map/ppermute | solution.py:126
  18.8 1.9 %collective-permute-start = (bf16[128,512]{1,0:T(8,128)(2,1)S(1)}, bf16[128,512]{1,0:T(8,128)(2,1)S(1)}, u32[]{:S(2)}, u32[]{:S(2)}) collective-permute-start(bf16[128,512]{1,0:T(8,128)(2,1)S(1)} %get-tuple-element.22), channel_id=1, source_target_pairs={{0,1},{1,2},{2,3},{3,4},{4,5},{5,6},{6,7},{7,8},{8,9},{9,10},{10,1... | collective-permute-start | bytes 393224 | tf_op jit(solution)/shard_map/ppermute | solution.py:125
  20.8 3.1 %early.1 = (bf16[512,1024]{1,0:T(8,128)(2,1)}, bf16[8,256,128]{2,1,0:T(8,128)(2,1)}, bf16[1024,256]{1,0:T(8,128)(2,1)}) custom-call(bf16[1024,512]{1,0:T(8,128)(2,1)} %refs_3_.1, bf16[512,256]{1,0:T(8,128)(2,1)} %refs_8_.1), custom_call_target="tpu_custom_call" | custom-call | flops 805306368 | bytes 4194304 | tf_op jit(solution)/shard_map/early/pallas_call | solution.py:150
  23.9 0.0 collective-permute-done.1.refs_5_
  23.9 0.0 copy-start
  23.9 5.5 %collective-permute-done.refs_4_ = bf16[128,512]{1,0:T(8,128)(2,1)S(1)} collective-permute-done((bf16[128,512]{1,0:T(8,128)(2,1)S(1)}, bf16[128,512]{1,0:T(8,128)(2,1)S(1)}, u32[]{:S(2)}, u32[]{:S(2)}) %collective-permute-start) | collective-permute-done | bytes 131104 | tf_op jit(solution)/shard_map/ppermute | solution.py:125
  29.3 0.0 copy-start.1
  29.3 0.0 copy-done
  29.3 0.7 copy-done.1
  30.0 6.0 %late.1 = (bf16[8,528,128]{2,1,0:T(8,128)(2,1)}, bf16[1024,256]{1,0:T(8,128)(2,1)}) custom-call(s32[8,8]{1,0:T(8,128)} %refs_0_.3, s32[8]{0:T(128)} %refs_1_.3, bf16[8,8,128,128]{3,2,1,0:T(8,128)(2,1)} %refs_2_.1, bf16[1024,512]{1,0:T(8,128)(2,1)} %refs_3_.1, bf16[128,512]{1,0:T(8,128)(2,1)} %copy-done.1, bf16[128,512]{1,0:T(8,128)(2,1)} %copy-done, ...), custom_call_target="tpu_custom_call" | custom-call | flops 2147483648 | bytes 8388608 | tf_op jit(solution)/shard_map/late/pallas_call | solution.py:165
  36.0 18.9 %all_to_all.15.in_ref = bf16[8,528,128]{2,1,0:T(8,128)(2,1)} all-to-all(bf16[8,528,128]{2,1,0:T(8,128)(2,1)} %get-tuple-element.17), channel_id=1, replica_groups=mesh['rows_0'=4,'rows_1'=8,'rows_2'=2,'cols'=12] {'rows_0','rows_2'}, dimensions={0} | all-to-all | bytes 2162688 | tf_op jit(solution)/shard_map/all_to_all | solution.py:131
  54.9 2.0 %split.1 = bf16[8,80,128]{2,1,0:T(8,128)(2,1)} custom-call(bf16[8,528,128]{2,1,0:T(8,128)(2,1)} %all_to_all.15.in_ref), custom_call_target="tpu_custom_call" | custom-call | tf_op jit(solution)/shard_map/split/pallas_call | solution.py:188
  56.9 14.1 %all_to_all.16.in_ref = bf16[8,80,128]{2,1,0:T(8,128)(2,1)} all-to-all(bf16[8,80,128]{2,1,0:T(8,128)(2,1)} %split.1), channel_id=1, replica_groups=mesh['rows_0'=4,'rows_1'=8,'rows_2'=2,'cols'=12] {'rows_1'}, dimensions={0} | all-to-all | bytes 327680 | tf_op jit(solution)/shard_map/all_to_all | solution.py:131
  71.1 1.6 %repeated.1 = bf16[12,80,128]{2,1,0:T(8,128)(2,1)} custom-call(bf16[8,80,128]{2,1,0:T(8,128)(2,1)} %all_to_all.16.in_ref), custom_call_target="tpu_custom_call" | custom-call | tf_op jit(solution)/shard_map/repeated/pallas_call | solution.py:195
  72.7 18.5 %all_to_all.17.refs_0_ = bf16[12,80,128]{2,1,0:T(8,128)(2,1)} all-to-all(bf16[12,80,128]{2,1,0:T(8,128)(2,1)} %repeated.1), channel_id=1, replica_groups=mesh['rows_0'=4,'rows_1'=8,'rows_2'=2,'cols'=12] {'cols'}, dimensions={0} | all-to-all | bytes 491520 | tf_op jit(solution)/shard_map/all_to_all | solution.py:131
  91.2 1.6 %final.1 = (f32[8,512]{1,0:T(8,128)}, f32[8,512]{1,0:T(8,128)}, f32[2,128]{1,0:T(2,128)}) custom-call(bf16[12,80,128]{2,1,0:T(8,128)(2,1)} %all_to_all.17.refs_0_), custom_call_target="tpu_custom_call" | custom-call | tf_op jit(solution)/shard_map/final/pallas_call | solution.py:202
Async XLA Ops:
  1.6 22.3 %collective-permute-start.1 = (bf16[128,512]{1,0:T(8,128)(2,1)S(1)}, bf16[128,512]{1,0:T(8,128)(2,1)S(1)}, u32[]{:S(2)}, u32[]{:S(2)}) collective-permute-start(bf16[128,512]{1,0:T(8,128)(2,1)S(1)} %get-tuple-element.21), channel_id=1, source_target_pairs={{1,0},{2,1},{3,2},{4,3},{5,4},{6,5},{7,6},{8,7},{9,8},{10,9},{11,1... | collective-permute-start | bytes 393224 | tf_op jit(solution)/shard_map/ppermute | solution.py:126
  18.8 10.5 %collective-permute-start = (bf16[128,512]{1,0:T(8,128)(2,1)S(1)}, bf16[128,512]{1,0:T(8,128)(2,1)S(1)}, u32[]{:S(2)}, u32[]{:S(2)}) collective-permute-start(bf16[128,512]{1,0:T(8,128)(2,1)S(1)} %get-tuple-element.22), channel_id=1, source_target_pairs={{0,1},{1,2},{2,3},{3,4},{4,5},{5,6},{6,7},{7,8},{8,9},{9,10},{10,1... | collective-permute-start | bytes 393224 | tf_op jit(solution)/shard_map/ppermute | solution.py:125
  23.9 5.5 %copy-start = (bf16[128,512]{1,0:T(8,128)(2,1)}, bf16[128,512]{1,0:T(8,128)(2,1)S(1)}, u32[]{:S(2)}) copy-start(bf16[128,512]{1,0:T(8,128)(2,1)S(1)} %collective-permute-done.1.refs_5_) | copy-start | bytes 393220
  29.3 0.7 copy-start.1

commit v2 on v1

v2 whole, which is shorter than its diff:
```python
import jax
import jax.numpy as jnp
from jax import lax
from jax.experimental import pallas as pl
from jax.experimental.pallas import tpu as pltpu
from jax.sharding import Mesh
from jax.sharding import PartitionSpec as P

ROWS = ("rows_0", "rows_1", "rows_2")
ROWS_COLS = ("rows_0", "rows_1", "rows_2", "cols")
LANES = 128
F32 = jnp.float32
BF16 = jnp.bfloat16


def dot(a, b):
    return jnp.dot(a, b, preferred_element_type=F32)


def store_tiles(out_ref, acc_ref, nx, ny, nc, core, first):
    tiles = acc_ref.shape[1] // LANES
    for x in range(nx):
        for y in range(ny):
            row = pl.multiple_of(((x * ny + y) * nc + core) * 8, 8)
            for j in range(0, tiles, 2):
                pair = jnp.concatenate(
                    [
                        acc_ref[pl.ds(row, 8), j * LANES : (j + 1) * LANES],
                        acc_ref[pl.ds(row, 8), (j + 1) * LANES : (j + 2) * LANES],
                    ],
                    axis=0,
                )
                at = (first + j) * 8
                out_ref[x, y, at : at + 16, :] = pair.astype(BF16)


def edges_kernel(basis_ref, held_ref, bottom_ref, top_ref):
    size = bottom_ref.shape[0]
    rows = basis_ref.shape[0]
    held_ref[...] = basis_ref[...]
    bottom_ref[...] = basis_ref[rows - size :, :]
    top_ref[...] = basis_ref[0:size, :]


def early_kernel(nx, ny, nc, basis_ref, basis_t_ref, own_ref, other_ref, acc_ref):
    basis_t_ref[...] = basis_ref[...].T
    acc_ref[...] = dot(basis_t_ref[...], basis_ref[...])
    core = lax.axis_index("rows_2")
    store_tiles(own_ref, acc_ref, nx, ny, nc, core, 0)
    store_tiles(other_ref, acc_ref, nx, ny, nc, nc - 1 - core, 0)


def late_kernel(
    nx, ny, nc,
    neighbours_ref, counts_ref, blocks_ref, basis_ref, low_ref, high_ref, basis_t_ref,
    own_gram_ref, other_gram_ref, rot_ref, values_ref, own_ref, other_ref, image_ref, padded_ref,
    acc_ref,
):
    nb, slots, size, _ = blocks_ref.shape
    rows, width = basis_ref.shape
    padded_ref[0:size, :] = low_ref[...]
    padded_ref[size : size + rows, :] = basis_ref[...]
    padded_ref[size + rows :, :] = high_ref[...]
    first = neighbours_ref[0, 0] - 1
    for b in range(nb):
        total = None
        for j in range(0, slots, 2):
            held = []
            picked = []
            for s in (j, j + 1):
                block = blocks_ref[b, s]
                held.append(jnp.where(s < counts_ref[b], block, jnp.zeros_like(block)))
                index = jnp.clip(neighbours_ref[b, s] - first, 0, nb + 1)
                picked.append(padded_ref[pl.ds(pl.multiple_of(index * size, size), size), :])
            part = dot(jnp.concatenate(held, axis=1), jnp.concatenate(picked, axis=0))
            total = part if total is None else total + part
        image_ref[b * size : (b + 1) * size, :] = total.astype(BF16)
    acc_ref[...] = dot(basis_t_ref[...], image_ref[...])
    tiles = width // LANES
    core = lax.axis_index("rows_2")
    own_ref[:, :, 0 : tiles * 8, :] = own_gram_ref[...]
    other_ref[:, :, 0 : tiles * 8, :] = other_gram_ref[...]
    store_tiles(own_ref, acc_ref, nx, ny, nc, core, tiles)
    store_tiles(other_ref, acc_ref, nx, ny, nc, nc - 1 - core, tiles)
    image_full = dot(image_ref[...], rot_ref[...])
    resid = image_full - values_ref[...] * dot(basis_ref[...], rot_ref[...])
    squares = jnp.sum(resid * resid, axis=0, keepdims=True)
    line = lax.broadcasted_iota(jnp.int32, (8, LANES), 0)
    spread = jnp.zeros((8, LANES), F32)
    for p in range(squares.shape[1] // LANES):
        spread = jnp.where(line == p, squares[:, p * LANES : (p + 1) * LANES], spread)
    lines = jnp.broadcast_to(spread.astype(BF16), (nx, ny, 8, LANES))
    own_ref[:, :, 2 * tiles * 8 :, :] = lines
    other_ref[:, :, 2 * tiles * 8 :, :] = lines


def final_kernel(rows_total, in_ref, gram_ref, projected_ref, res_ref):
    total = in_ref[0].astype(F32)
    for i in range(1, in_ref.shape[0]):
        total = total + in_ref[i].astype(F32)
    total = total / rows_total
    tiles = gram_ref.shape[1] // LANES
    for j in range(tiles):
        gram_ref[:, j * LANES : (j + 1) * LANES] = total[j * 8 : (j + 1) * 8]
        projected_ref[:, j * LANES : (j + 1) * LANES] = total[(tiles + j) * 8 : (tiles + j + 1) * 8]
    res_ref[...] = jnp.sqrt(total[2 * tiles * 8 : 2 * tiles * 8 + res_ref.shape[0]])


def halos(bottom, top):
    count = lax.axis_size(ROWS_COLS)
    forward = [(i, i + 1) for i in range(count - 1)]
    backward = [(target, source) for source, target in forward]
    low = lax.ppermute(bottom, ROWS_COLS, forward)
    high = lax.ppermute(top, ROWS_COLS, backward)
    return low, high


def room(mib):
    return pltpu.CompilerParams(vmem_limit_bytes=mib * 2**20)


def exchanged(x, axes):
    return lax.all_to_all(x, axes, split_axis=0, concat_axis=0, tiled=True)


def summed(x, axes):
    arrived = exchanged(x, axes)
    total = arrived[0].astype(F32)
    for i in range(1, arrived.shape[0]):
        total = total + arrived[i].astype(F32)
    return total


def shape(dims, dtype):
    return jax.ShapeDtypeStruct(dims, dtype)


def body(basis, blocks, neighbours, counts, rotation, ritz_values):
    rows, width = basis.shape
    size = blocks.shape[2]
    kept = rotation.shape[1]
    nx, ny, nc = (lax.axis_size(axis) for axis in ROWS)
    nz = lax.axis_size("cols")
    rows_total = rows * nx * ny * nc * nz
    tiles = width // LANES
    vmem = pl.BlockSpec(memory_space=pltpu.VMEM)
    smem = pl.BlockSpec(memory_space=pltpu.SMEM)
    held, bottom, top = pl.pallas_call(
        edges_kernel,
        out_shape=(shape(basis.shape, BF16), shape((size, width), BF16), shape((size, width), BF16)),
        in_specs=[vmem],
        out_specs=(vmem,) * 3,
        compiler_params=room(8),
        name="edges",
    )(basis)
    low, high = halos(bottom, top)
    basis_t, own_gram, other_gram = pl.pallas_call(
        lambda *refs: early_kernel(nx, ny, nc, *refs),
        out_shape=(
            shape((width, rows), BF16),
            shape((nx, ny, tiles * 8, LANES), BF16),
            shape((nx, ny, tiles * 8, LANES), BF16),
        ),
        in_specs=[vmem],
        out_specs=(vmem,) * 3,
        scratch_shapes=[pltpu.VMEM((width, width), F32)],
        cost_estimate=pl.CostEstimate(
            flops=2 * rows * width * width, bytes_accessed=4 * rows * width * 2, transcendentals=0
        ),
        name="early",
        compiler_params=room(16),
    )(held)
    each = 2 * tiles * 8 + 8
    own, other, image = pl.pallas_call(
        lambda *refs: late_kernel(nx, ny, nc, *refs),
        out_shape=(
            shape((nx, ny, each, LANES), BF16),
            shape((nx, ny, each, LANES), BF16),
            shape((rows, width), BF16),
        ),
        in_specs=[smem, smem] + [vmem] * 9,
        out_specs=(vmem,) * 3,
        scratch_shapes=[
            pltpu.VMEM((rows + 2 * size, width), BF16),
            pltpu.VMEM((width, width), F32),
        ],
        cost_estimate=pl.CostEstimate(
            flops=4 * rows * width * 1024, bytes_accessed=8 * rows * width * 2, transcendentals=0
        ),
        name="late",
        compiler_params=room(20),
    )(
        neighbours, counts, blocks, held, low, high, basis_t, own_gram, other_gram, rotation,
        ritz_values.reshape(1, kept),
    )
    ritz = dot(held, rotation).astype(BF16)
    ritz_image = dot(image, rotation).astype(BF16)
    partner = lax.ppermute(other, "rows_2", [(i, nc - 1 - i) for i in range(nc)])
    part = (own.astype(F32) + partner.astype(F32)).astype(BF16)
    part = summed(part, "rows_0").astype(BF16)
    part = summed(part, "rows_1").astype(BF16)
    every = exchanged(jnp.broadcast_to(part[None], (nz, each, LANES)), "cols")
    gram, projected, res = pl.pallas_call(
        lambda *refs: final_kernel(rows_total, *refs),
        out_shape=(
            shape((8, width), F32),
            shape((8, width), F32),
            shape((kept // LANES, LANES), F32),
        ),
        in_specs=[vmem],
        out_specs=(vmem,) * 3,
        compiler_params=room(8),
        name="final",
    )(every)
    return ritz, ritz_image, gram, projected, res.reshape(kept)


def solution(mesh):
    finer = Mesh(
        mesh.devices.reshape(4, 8, 2, mesh.shape["cols"]), ("rows_0", "rows_1", "rows_2", "cols")
    )
    return jax.shard_map(
        body,
        mesh=finer,
        in_specs=(
            P(ROWS_COLS, None),
            P(ROWS_COLS, None, None, None),
            P(ROWS_COLS, None),
            P(ROWS_COLS),
            P(),
            P(),
        ),
        out_specs=(P(ROWS_COLS, None), P(ROWS_COLS, None), P(ROWS, None), P(ROWS, None), P()),
        check_vma=False,
    )
```

time: 94.3 us -> 81 us (0.86)
  blocking collectives: 51.5 us -> 27.3 us
  Pallas kernels: 14.4 us -> 4.72 us
  waiting for transfers between devices: 5.45 us -> 14.5 us
  starting transfers between devices: 19.1 us -> 28 us
  matrix products: 0 us -> 2.46 us
    all_to_all x3 -> x2, blocking collectives: 51.5 us -> 27.3 us  [exchanged(): return lax.all_to_all(x, axes, split_axis=0, concat_axis=0, tiled=True)]
    all_to_all x0 -> x1, waiting for transfers between devices: none -> 10.8 us  [exchanged(): return lax.all_to_all(x, axes, split_axis=0, concat_axis=0, tiled=True)]
    all_to_all x0 -> x1, starting transfers between devices: none -> 6.82 us  [exchanged(): return lax.all_to_all(x, axes, split_axis=0, concat_axis=0, tiled=True)]
    pallas_call x2 -> x1, Pallas kernels: 3.66 us -> 0.09 us  [body(): pl.pallas_call(edges_kernel, out_shape=(shape(basis.shape, BF16), shape((...]
    pallas_call x1, Pallas kernels: 6.04 us -> 3.18 us  [body(): pl.pallas_call(lambda *refs: late_kernel(nx, ny, nc, *refs), out_shape=(s...]
    dot_general x0 -> x2, matrix products: none -> 2.46 us  [dot(): return jnp.dot(a, b, preferred_element_type=F32)]
    pallas_call x1, Pallas kernels: 3.12 us -> 0.81 us  [body(): pl.pallas_call(lambda *refs: early_kernel(nx, ny, nc, *refs), out_shape=(...]
    ppermute x2 -> x3, starting transfers between devices: 19.1 us -> 21.2 us  [the longest x1 14.8 us: halos(): high = lax.ppermute(top, ROWS_COLS, backward)]
  transfers between devices with their start and end apart: 2 -> 4, of which waited for: 1 -> 4; matrix products, arithmetic and copies ran while one was open for 0% -> 3% of each run, Pallas kernels for 3% -> 1%
where the time goes in v2:
time: 81 us; the launch traced here: 79.9 us
  starting transfers between devices  28 us (35%)
  blocking collectives  27.3 us (34%)
  waiting for transfers between devices  14.5 us (18%)
  Pallas kernels  4.72 us (6%)
  matrix products  2.46 us (3%)
  local copies, waits for them, and re-layouts  1.96 us (2%)
    all_to_all x2, blocking collectives, exchanged(): return lax.all_to_all(x, axes, split_axis=0, concat_axis=0, tiled=True)  27.3 us
    ppermute x1, starting transfers between devices, halos(): high = lax.ppermute(top, ROWS_COLS, backward)  14.8 us
    all_to_all x1, waiting for transfers between devices, exchanged(): return lax.all_to_all(x, axes, split_axis=0, concat_axis=0, tiled=True)  10.8 us
    all_to_all x1, starting transfers between devices, exchanged(): return lax.all_to_all(x, axes, split_axis=0, concat_axis=0, tiled=True)  6.82 us
    ppermute x1, starting transfers between devices, halos(): low = lax.ppermute(bottom, ROWS_COLS, forward)  4.41 us
    pallas_call x1, Pallas kernels, body(): pl.pallas_call(lambda *refs: late_kernel(nx, ny, nc, *refs), out_shape=(s...  3.18 us
    dot_general x2, matrix products, dot(): return jnp.dot(a, b, preferred_element_type=F32)  2.46 us
    ppermute x1, waiting for transfers between devices, body(): lax.ppermute(other, 'rows_2', [(i, nc - 1 - i) for i in range(nc)])  1.97 us
  transfers between devices with their start and end apart: 4, of which 4 were waited for; matrix products, arithmetic and copies ran while one was open for 3% of the time, Pallas kernels for 1%

profile of v2, /device:TPU:6, one launch (start us, length us, event | category | flops | bytes accessed | tf_op | source)
XLA Modules:
  0.0 79.9 jit_solution(8662696394908949849)
XLA Ops:
  0.6 0.0 copy-start.1
  0.6 1.2 %copy-done.1 = bf16[1024,512]{1,0:T(8,128)(2,1)S(1)} copy-done((bf16[1024,512]{1,0:T(8,128)(2,1)S(1)}, bf16[1024,512]{1,0:T(8,128)(2,1)}, u32[]{:S(2)}) %copy-start.1) | copy-done | bytes 1048600
  1.9 0.0 copy-start.2
  1.9 0.1 edges.1
  1.9 0.0 copy-start
  2.0 0.0 copy-start.3
  2.0 0.0 copy-start.4
  2.0 0.0 copy-start.5
  2.0 4.4 %collective-permute-start = (bf16[128,512]{1,0:T(8,128)(2,1)S(1)}, bf16[128,512]{1,0:T(8,128)(2,1)S(1)}, u32[]{:S(2)}, u32[]{:S(2)}) collective-permute-start(bf16[128,512]{1,0:T(8,128)(2,1)S(1)} %get-tuple-element.18), channel_id=1, source_target_pairs={{0,1},{1,2},{2,3},{3,4},{4,5},{5,6},{6,7},{7,8},{8,9},{9,10},{10,1... | collective-permute-start | bytes 393224 | tf_op jit(solution)/shard_map/ppermute | solution.py:113
  6.4 14.8 %collective-permute-start.1 = (bf16[128,512]{1,0:T(8,128)(2,1)S(1)}, bf16[128,512]{1,0:T(8,128)(2,1)S(1)}, u32[]{:S(2)}, u32[]{:S(2)}) collective-permute-start(bf16[128,512]{1,0:T(8,128)(2,1)S(1)} %get-tuple-element.19), channel_id=1, source_target_pairs={{1,0},{2,1},{3,2},{4,3},{5,4},{6,5},{7,6},{8,7},{9,8},{10,9},{11,1... | collective-permute-start | bytes 393224 | tf_op jit(solution)/shard_map/ppermute | solution.py:114
  21.3 0.8 %early.1 = (bf16[512,1024]{1,0:T(8,128)(2,1)S(1)}, bf16[4,8,32,128]{3,2,1,0:T(8,128)(2,1)S(1)}, bf16[4,8,32,128]{3,2,1,0:T(8,128)(2,1)S(1)}) custom-call(bf16[1024,512]{1,0:T(8,128)(2,1)S(1)} %get-tuple-element.17.refs_0_.refs_3_), custom_call_target="tpu_custom_call" | custom-call | flops 536870912 | bytes 4194304 | tf_op jit(solution)/shard_map/early/pallas_call | solution.py:157
  22.1 0.4 collective-permute-done.refs_4_
  22.5 1.2 %collective-permute-done.1.refs_5_ = bf16[128,512]{1,0:T(8,128)(2,1)S(1)} collective-permute-done((bf16[128,512]{1,0:T(8,128)(2,1)S(1)}, bf16[128,512]{1,0:T(8,128)(2,1)S(1)}, u32[]{:S(2)}, u32[]{:S(2)}) %collective-permute-start.1) | collective-permute-done | bytes 131104 | tf_op jit(solution)/shard_map/ppermute | solution.py:114
  23.8 0.0 copy-done.2
  23.8 0.0 copy-done
  23.8 0.0 copy-done.3
  23.8 0.0 copy-done.4
  23.8 0.0 copy-done.5
  23.8 3.2 %late.1 = (bf16[4,8,72,128]{3,2,1,0:T(8,128)(2,1)S(1)}, bf16[4,8,72,128]{3,2,1,0:T(8,128)(2,1)S(1)}, bf16[1024,512]{1,0:T(8,128)(2,1)S(1)}) custom-call(s32[8,8]{1,0:T(8,128)S(1)} %copy-done.3, s32[8]{0:T(128)S(1)} %copy-done.5, bf16[8,8,128,128]{3,2,1,0:T(8,128)(2,1)S(1)} %copy-done.2, bf16[1024,512]{1,0:T(8,128)(2,1)S(1)} %get-tuple-element.17.refs_0_.refs_3_, ...), custom_call_target="tpu_custom_call" | custom-call | flops 2147483648 | bytes 8388608 | tf_op jit(solution)/shard_map/late/pallas_call | solution.py:174
  27.0 1.9 %collective-permute-start.2 = (bf16[4,8,72,128]{3,2,1,0:T(8,128)(2,1)S(1)}, bf16[4,8,72,128]{3,2,1,0:T(8,128)(2,1)S(1)}, u32[]{:S(2)}, u32[]{:S(2)}) collective-permute-start(bf16[4,8,72,128]{3,2,1,0:T(8,128)(2,1)S(1)} %get-tuple-element.25), channel_id=1, source_target_pairs={{0,12},{12,0},{1,13},{13,1},{2,14},{14,2},{3,15},{15,3},{4,16},{16... | collective-permute-start | bytes 1769480 | tf_op jit(solution)/shard_map/ppermute | solution.py:198
  28.9 2.0 %collective-permute-done.2 = bf16[4,8,72,128]{3,2,1,0:T(8,128)(2,1)S(1)} collective-permute-done((bf16[4,8,72,128]{3,2,1,0:T(8,128)(2,1)S(1)}, bf16[4,8,72,128]{3,2,1,0:T(8,128)(2,1)S(1)}, u32[]{:S(2)}, u32[]{:S(2)}) %collective-permute-start.2) | collective-permute-done | bytes 589856 | tf_op jit(solution)/shard_map/ppermute | solution.py:198
  30.9 0.2 add_convert_fusion
  31.0 12.7 %all_to_all.15 = bf16[4,8,72,128]{3,2,1,0:T(8,128)(2,1)S(1)} all-to-all(bf16[4,8,72,128]{3,2,1,0:T(8,128)(2,1)S(1)} %add_convert_fusion), channel_id=1, replica_groups=mesh['rows_0'=4,'rows_1'=8,'rows_2'=2,'cols'=12] {'rows_0'}, dimensions={0} | all-to-all | bytes 1179648 | tf_op jit(solution)/shard_map/all_to_all | solution.py:123
  43.8 0.1 fusion
  43.8 14.6 %all_to_all.16 = bf16[8,72,128]{2,1,0:T(8,128)(2,1)S(1)} all-to-all(bf16[8,72,128]{2,1,0:T(8,128)(2,1)S(1)} %fusion), channel_id=1, replica_groups=mesh['rows_0'=4,'rows_1'=8,'rows_2'=2,'cols'=12] {'rows_1'}, dimensions={0} | all-to-all | bytes 294912 | tf_op jit(solution)/shard_map/all_to_all | solution.py:123
  58.5 0.7 broadcast_in_dim.9
  59.2 6.8 %all-to-all-start.2 = ((bf16[12,72,128]{2,1,0:T(8,128)(2,1)}), bf16[12,72,128]{2,1,0:T(8,128)(2,1)S(1)}, u32[]{:S(2)}, u32[]{:S(2)}) async-start(bf16[12,72,128]{2,1,0:T(8,128)(2,1)} %broadcast_in_dim.9), calls=%async_computation.2 | async-start | bytes 442368 | tf_op jit(solution)/shard_map/all_to_all | solution.py:123
  66.0 1.2 %convolution_convert_fusion.1 = bf16[1024,256]{1,0:T(8,128)(2,1)} fusion(bf16[1024,512]{1,0:T(8,128)(2,1)S(1)} %get-tuple-element.17.refs_0_.refs_3_, bf16[512,256]{1,0:T(8,128)(2,1)S(1)} %copy-done), kind=kOutput, calls=%fused_computation.1 | convolution fusion | flops 268697600 | bytes 1835008 | tf_op jit(solution)/shard_map/dot_general | solution.py:17
  67.2 1.2 %convolution_convert_fusion = bf16[1024,256]{1,0:T(8,128)(2,1)} fusion(bf16[1024,512]{1,0:T(8,128)(2,1)S(1)} %get-tuple-element.23, bf16[512,256]{1,0:T(8,128)(2,1)S(1)} %copy-done), kind=kOutput, calls=%fused_computation | convolution fusion | flops 268697600 | bytes 1835008 | tf_op jit(solution)/shard_map/dot_general | solution.py:17
  68.5 10.8 %all-to-all-done.2.refs_0_ = bf16[12,72,128]{2,1,0:T(8,128)(2,1)S(1)} async-done(((bf16[12,72,128]{2,1,0:T(8,128)(2,1)}), bf16[12,72,128]{2,1,0:T(8,128)(2,1)S(1)}, u32[]{:S(2)}, u32[]{:S(2)}) %all-to-all-start.2) | async-done | bytes 221216 | tf_op jit(solution)/shard_map/all_to_all | solution.py:123
  79.3 0.6 final.1
  (1 shorter events, 0.0 us)
Async XLA Ops:
  0.6 1.2 %copy-start.1 = (bf16[1024,512]{1,0:T(8,128)(2,1)S(1)}, bf16[1024,512]{1,0:T(8,128)(2,1)}, u32[]{:S(2)}) copy-start(bf16[1024,512]{1,0:T(8,128)(2,1)} %basis_ref.1) | copy-start | bytes 3145732
  1.9 21.9 %copy-start.2 = (bf16[8,8,128,128]{3,2,1,0:T(8,128)(2,1)S(1)}, bf16[8,8,128,128]{3,2,1,0:T(8,128)(2,1)}, u32[]{:S(2)}) copy-start(bf16[8,8,128,128]{3,2,1,0:T(8,128)(2,1)} %refs_2_.1) | copy-start | bytes 6291460
  1.9 21.8 %copy-start = (bf16[512,256]{1,0:T(8,128)(2,1)S(1)}, bf16[512,256]{1,0:T(8,128)(2,1)}, u32[]{:S(2)}) copy-start(bf16[512,256]{1,0:T(8,128)(2,1)} %refs_9_.1) | copy-start | bytes 786436
  2.0 21.8 %copy-start.3 = (s32[8,8]{1,0:T(8,128)S(1)}, s32[8,8]{1,0:T(8,128)}, u32[]{:S(2)}) copy-start(s32[8,8]{1,0:T(8,128)} %refs_0_.1) | copy-start | bytes 772
  2.0 21.8 %copy-start.4 = (f32[256]{0:T(256)S(1)}, f32[256]{0:T(256)}, u32[]{:S(2)}) copy-start(f32[256]{0:T(256)} %param.11) | copy-start | bytes 3076
  2.0 21.8 %copy-start.5 = (s32[8]{0:T(128)S(1)}, s32[8]{0:T(128)}, u32[]{:S(2)}) copy-start(s32[8]{0:T(128)} %refs_1_.1) | copy-start | bytes 100
  2.0 20.5 %collective-permute-start = (bf16[128,512]{1,0:T(8,128)(2,1)S(1)}, bf16[128,512]{1,0:T(8,128)(2,1)S(1)}, u32[]{:S(2)}, u32[]{:S(2)}) collective-permute-start(bf16[128,512]{1,0:T(8,128)(2,1)S(1)} %get-tuple-element.18), channel_id=1, source_target_pairs={{0,1},{1,2},{2,3},{3,4},{4,5},{5,6},{6,7},{7,8},{8,9},{9,10},{10,1... | collective-permute-start | bytes 393224 | tf_op jit(solution)/shard_map/ppermute | solution.py:113
  6.4 17.3 %collective-permute-start.1 = (bf16[128,512]{1,0:T(8,128)(2,1)S(1)}, bf16[128,512]{1,0:T(8,128)(2,1)S(1)}, u32[]{:S(2)}, u32[]{:S(2)}) collective-permute-start(bf16[128,512]{1,0:T(8,128)(2,1)S(1)} %get-tuple-element.19), channel_id=1, source_target_pairs={{1,0},{2,1},{3,2},{4,3},{5,4},{6,5},{7,6},{8,7},{9,8},{10,9},{11,1... | collective-permute-start | bytes 393224 | tf_op jit(solution)/shard_map/ppermute | solution.py:114
  27.0 3.9 %collective-permute-start.2 = (bf16[4,8,72,128]{3,2,1,0:T(8,128)(2,1)S(1)}, bf16[4,8,72,128]{3,2,1,0:T(8,128)(2,1)S(1)}, u32[]{:S(2)}, u32[]{:S(2)}) collective-permute-start(bf16[4,8,72,128]{3,2,1,0:T(8,128)(2,1)S(1)} %get-tuple-element.25), channel_id=1, source_target_pairs={{0,12},{12,0},{1,13},{13,1},{2,14},{14,2},{3,15},{15,3},{4,16},{16... | collective-permute-start | bytes 1769480 | tf_op jit(solution)/shard_map/ppermute | solution.py:198
  59.2 20.1 %all-to-all-start.2 = ((bf16[12,72,128]{2,1,0:T(8,128)(2,1)}), bf16[12,72,128]{2,1,0:T(8,128)(2,1)S(1)}, u32[]{:S(2)}, u32[]{:S(2)}) async-start(bf16[12,72,128]{2,1,0:T(8,128)(2,1)} %broadcast_in_dim.9), calls=%async_computation.2 | async-start | bytes 442368 | tf_op jit(solution)/shard_map/all_to_all | solution.py:123
